TPU v7x, 32 devices: a whole 2x2x4 slice. The times are simulated.
32 devices in a mesh: seq: 16 (over z, y, core), head: 2 (over x).
Axes of the slice: x: 2, y: 2, z: 4, core: 2. Of those that a mesh axis runs over, the one named last changes fastest.
Arguments:
- query: bfloat16 [1024, 5120], P('seq', 'head'), may hold values from -3 to 3
- query_offset: int32 [1024], P('seq'), may hold values from 0 to 255
- attn_out: bfloat16 [1024, 5120], P('seq', 'head'), may hold values from -3 to 3
- out_grad: bfloat16 [1024, 5120], P('seq', 'head'), may hold values from -24 to 24
- log_norm: float32 [40, 1024], P('head', 'seq'), may hold values from 4 to 6
- keys: bfloat16 [4096, 5120], P('seq', 'head'), may hold values from -6 to 6
- values: bfloat16 [4096, 5120], P('seq', 'head'), may hold values from -6 to 6
Outputs:
- key_grad: bfloat16 [4096, 5120], P('seq', 'head')
- value_grad: bfloat16 [4096, 5120], P('seq', 'head')
- query_grad: bfloat16 [1024, 5120], P(('seq', 'head'))
All inputs are finite; a program needn't handle non-finite values.
Results may differ from a plain program's by a relative error of at most 0.0051.
Values may be sent and summed in bfloat16 or wider, within the bound.
A program may use at most 64 MiB of HBM per device.

v0:
```python
import functools
import math

import jax
import jax.numpy as jnp
from jax import lax
from jax.experimental import pallas as pl
from jax.experimental.pallas import tpu as pltpu
from jax.sharding import PartitionSpec as P

STEPS = 4
HEADS_PER_CHUNK = 2
F32 = jnp.float32
BF16 = jnp.bfloat16


def dot(a, b, ca, cb):
    return lax.dot_general(a, b, (((ca,), (cb,)), ((), ())), preferred_element_type=F32)


def kernel(
    dims, q_hbm, off_hbm, o_hbm, do_hbm, ln_hbm, k_hbm, v_hbm,
    kg_hbm, vg_hbm, qg_hbm,
    x, kb, vb, ob, lnb, offb, st, lse, dlt, offrow, own, part, got, fin, kgb, vgb, outb,
    load_sem, kv_sem, small_sem, xs, xr, ss, sr, ps, pr, fs, fr, out_sem, last_sem,
):
    n, hn, heads, hc, dh, qb, kbr = dims
    chunks = heads // hc
    w = hc * dh
    feats = heads * dh
    rows_out = qb // hn
    scale = 1.0 / math.sqrt(dh)
    me = lax.axis_index("seq")
    hd = lax.axis_index("head")
    k = lax.rem(me, 2)
    partner = me + 1 - 2 * k
    oa = 1 + 2 * k
    oc = 3 - 2 * k
    has2 = me + 2 < n
    hasa = me + oa < n
    to2 = me >= 2
    toc = me >= oc
    quad = lax.rem(me, 4)
    by_relay = quad == 0
    send2 = to2 & jnp.logical_not(by_relay)
    hops = (quad == 1) & hasa
    below = (quad == 2) & has2

    def rows(o):
        return pl.ds(pl.multiple_of(o * qb, qb), qb)

    def cols(g):
        return pl.ds(pl.multiple_of(g * w, w), w)

    def load_q(g):
        return pltpu.make_async_copy(q_hbm.at[:, cols(g)], x.at[g, 0, pl.ds(0, qb)], load_sem.at[0, g])

    def load_do(g):
        return pltpu.make_async_copy(do_hbm.at[:, cols(g)], x.at[g, 1, pl.ds(0, qb)], load_sem.at[1, g])

    def load_k(g):
        return pltpu.make_async_copy(k_hbm.at[:, cols(g)], kb.at[g], kv_sem.at[0, g])

    def load_v(g):
        return pltpu.make_async_copy(v_hbm.at[:, cols(g)], vb.at[g], kv_sem.at[1, g])

    load_o = pltpu.make_async_copy(o_hbm, ob, small_sem.at[0])
    load_ln = pltpu.make_async_copy(ln_hbm, lnb, small_sem.at[1])
    load_off = pltpu.make_async_copy(off_hbm, offb, small_sem.at[2])

    def remote(src, dst, send, recv, target):
        return pltpu.make_async_remote_copy(
            src_ref=src, dst_ref=dst, send_sem=send, recv_sem=recv,
            device_id={"seq": target}, device_id_type=pl.DeviceIdType.MESH,
        )

    def x_direct2(g):
        return remote(x.at[g, :, pl.ds(0, qb)], x.at[g, :, rows(2)], xs.at[0, g], xr.at[0, g], me - 2)

    def x_directc(g):
        return remote(x.at[g, :, pl.ds(0, qb)], x.at[g, :, rows(oc)], xs.at[1, g], xr.at[1, g], me - oc)

    def x_relay(g):
        return remote(x.at[g, :, rows(2)], x.at[g, :, rows(oa)], xs.at[2, g], xr.at[2, g], partner)

    def x_hop(g):
        return remote(x.at[g, :, rows(oa)], x.at[g, :, rows(2)], xs.at[0, g], xr.at[0, g], me + 1)

    st_direct2 = remote(st.at[0], st.at[2], ss.at[0], sr.at[0], me - 2)
    st_directc = remote(st.at[0], st.at[oc], ss.at[1], sr.at[1], me - oc)
    st_relay = remote(st.at[2], st.at[oa], ss.at[2], sr.at[2], partner)

    def p_partner(g):
        return remote(part.at[g, rows(oc)], got.at[0, g], ps.at[0, g], pr.at[0, g], partner)

    def p_ahead(g):
        return remote(part.at[g, rows(oa)], got.at[1, g], ps.at[1, g], pr.at[1, g], me + oa)

    def p_two(g):
        return remote(part.at[g, rows(2)], got.at[2, g], ps.at[2, g], pr.at[2, g], me + 2)

    def f_send(g, d):
        peer = lax.rem(hd + d, hn)
        return pltpu.make_async_remote_copy(
            src_ref=fin.at[g, pl.ds(pl.multiple_of(peer * rows_out, rows_out), rows_out)],
            dst_ref=outb.at[:, pl.ds(pl.multiple_of(hd * feats + g * w, w), w)],
            send_sem=fs.at[d - 1, g], recv_sem=fr.at[d - 1, g],
            device_id={"head": peer}, device_id_type=pl.DeviceIdType.MESH,
        )

    @pl.loop(0, chunks)
    def _(g):
        load_q(g).start()
        load_do(g).start()

    load_ln.start()
    load_off.start()
    load_o.start()

    @pl.loop(0, chunks)
    def _(g):
        load_k(g).start()
        load_v(g).start()

    barrier = pltpu.get_barrier_semaphore()
    far = me + 6 * k - 3
    has_far = (far >= 0) & (far < n)

    def greet(target):
        pl.semaphore_signal(barrier, inc=1, device_id={"seq": target}, device_id_type=pl.DeviceIdType.MESH)

    greet(partner)
    for d in range(1, hn):
        pl.semaphore_signal(
            barrier, inc=1, device_id={"head": lax.rem(hd + d, hn)}, device_id_type=pl.DeviceIdType.MESH
        )
    pl.when(to2)(lambda: greet(me - 2))
    pl.when(has2)(lambda: greet(me + 2))
    pl.when(has_far)(lambda: greet(far))
    pl.when(hops)(lambda: greet(me + 1))
    pl.when(below)(lambda: greet(me - 1))
    peers = hn + to2.astype(jnp.int32) + has2.astype(jnp.int32) + has_far.astype(jnp.int32)
    peers = peers + hops.astype(jnp.int32) + below.astype(jnp.int32)
    pl.semaphore_wait(barrier, peers)

    def wait_x(g):
        load_q(g).wait()
        load_do(g).wait()

    def send_x(g):
        pl.when(send2)(lambda: x_direct2(g).start())
        pl.when(toc)(lambda: x_directc(g).start())

    wait_x(0)
    send_x(0)

    load_ln.wait()
    load_off.wait()
    load_o.wait()
    st[0, :, 0:qb] = lnb[...]
    eye = lax.broadcasted_iota(jnp.int32, (qb, qb), 0) == lax.broadcasted_iota(jnp.int32, (qb, qb), 1)

    @pl.loop(0, chunks)
    def _(g):
        pl.when(g > 0)(lambda: wait_x(g))
        for h in range(hc):
            oh = ob[:, pl.ds(pl.multiple_of(g * w + h * dh, dh), dh)]
            doh = x[g, 1, 0:qb, h * dh:(h + 1) * dh]
            t = dot(oh, doh, 1, 1)
            st[0, pl.ds(g * hc + h, 1), qb:2 * qb] = jnp.sum(jnp.where(eye, t, 0.0), axis=0, keepdims=True)

    pl.when(to2)(lambda: st_direct2.start())
    pl.when(toc)(lambda: st_directc.start())

    @pl.loop(1, chunks)
    def _(g):
        send_x(g)

    def zero_rows(o):
        @pl.loop(0, chunks)
        def _(g):
            for i in range(2):
                x[g, i, rows(o), :] = jnp.zeros((qb, w), BF16)
        st[o] = jnp.zeros_like(st[o])

    @pl.when(jnp.logical_not(has2))
    def _():
        zero_rows(2)
        zero_rows(oc)

    @pl.when(jnp.logical_not(hasa))
    def _():
        zero_rows(oa)

    offrow[...] = jnp.full(offrow.shape, kbr, jnp.int32)
    offrow[:, 0:qb] = offb[...]

    def relay(g):
        pl.when(hasa)(lambda: x_directc(g).wait_recv())
        pl.when(hops)(lambda: x_hop(g).start())

        @pl.when(has2)
        def _():
            x_direct2(g).wait_recv()
            x_relay(g).start()

    def compute(g):
        pl.when(has2)(lambda: x_relay(g).wait_recv())
        load_k(g).wait()
        load_v(g).wait()
        allowed = lax.broadcasted_iota(jnp.int32, (kbr, STEPS * qb), 0) <= offrow[...]
        for h in range(hc):
            c = slice(h * dh, (h + 1) * dh)
            qh = x[g, 0, :, c]
            doh = x[g, 1, :, c]
            kh = kb[g, :, c]
            vh = vb[g, :, c]
            row = pl.ds(g * hc + h, 1)
            s = dot(kh, qh, 1, 1) * scale - lse[row, :]
            p = jnp.where(allowed, jnp.exp(s), 0.0)
            dp = dot(vh, doh, 1, 1)
            ds = (p * (dp - dlt[row, :]) * scale).astype(BF16)
            vgb[g, :, c] = dot(p.astype(BF16), doh, 1, 0).astype(BF16)
            kgb[g, :, c] = dot(ds, qh, 1, 0).astype(BF16)
            dq = dot(ds, kh, 0, 0)
            own[g, :, c] = dq
            part[g, :, c] = dq.astype(BF16)
        pl.when(has2)(lambda: p_partner(g).start())
        pl.when(hasa)(lambda: p_ahead(g).start())
        out_k(g).start()
        out_v(g).start()

    def out_k(g):
        return pltpu.make_async_copy(kgb.at[g], kg_hbm.at[:, cols(g)], out_sem.at[0, g])

    def out_v(g):
        return pltpu.make_async_copy(vgb.at[g], vg_hbm.at[:, cols(g)], out_sem.at[1, g])

    def combine(g):
        @pl.when(has2)
        def _():
            p_partner(g).wait_recv()
            both = own[g, 2 * qb:3 * qb, :] + got[0, g].astype(F32)
            part[g, 2 * qb:3 * qb, :] = both.astype(BF16)
            p_two(g).start()

    def finish(g):
        @pl.when(to2)
        def _():
            p_two(g).wait_recv()
            own[g, 0:qb, :] = own[g, 0:qb, :] + got[2, g].astype(F32)

        @pl.when(toc)
        def _():
            p_ahead(g).wait_recv()
            own[g, 0:qb, :] = own[g, 0:qb, :] + got[1, g].astype(F32)

        fin[g] = own[g, 0:qb, :].astype(BF16)
        for d in range(1, hn):
            f_send(g, d).start()
        outb[:, pl.ds(pl.multiple_of(hd * feats + g * w, w), w)] = fin[
            g, pl.ds(pl.multiple_of(hd * rows_out, rows_out), rows_out), :
        ]

    relay(0)

    @pl.when(has2)
    def _():
        st_direct2.wait_recv()
        st_relay.start()

    pl.when(hasa)(lambda: st_directc.wait_recv())
    pl.when(has2)(lambda: st_relay.wait_recv())
    for o in range(STEPS):
        lse[:, o * qb:(o + 1) * qb] = st[o, :, 0:qb]
        dlt[:, o * qb:(o + 1) * qb] = st[o, :, qb:2 * qb]

    @pl.loop(1, chunks + 2)
    def _(t):
        pl.when(t < chunks)(lambda: relay(t))
        pl.when(t <= chunks)(lambda: compute(t - 1))
        pl.when(t >= 2)(lambda: combine(t - 2))

    @pl.loop(0, chunks)
    def _(g):
        finish(g)

    @pl.loop(0, chunks)
    def _(g):
        for d in range(1, hn):
            f_send(g, d).wait()

    last = pltpu.make_async_copy(outb, qg_hbm, last_sem)
    last.start()

    @pl.loop(0, chunks)
    def _(g):
        pl.when(send2)(lambda: x_direct2(g).wait_send())
        pl.when(hops)(lambda: x_hop(g).wait_send())
        pl.when(toc)(lambda: x_directc(g).wait_send())

        @pl.when(has2)
        def _():
            x_relay(g).wait_send()
            p_partner(g).wait_send()
            p_two(g).wait_send()

        pl.when(hasa)(lambda: p_ahead(g).wait_send())
        out_k(g).wait()
        out_v(g).wait()

    pl.when(to2)(lambda: st_direct2.wait_send())
    pl.when(toc)(lambda: st_directc.wait_send())
    pl.when(has2)(lambda: st_relay.wait_send())
    last.wait()


def per_device(query, query_offset, attn_out, out_grad, log_norm, keys, values):
    n = lax.axis_size("seq")
    hn = lax.axis_size("head")
    heads = log_norm.shape[0]
    qb, feats = query.shape
    kbr = keys.shape[0]
    dh = feats // heads
    hc = HEADS_PER_CHUNK
    while heads % hc:
        hc -= 1
    chunks = heads // hc
    w = hc * dh
    dims = (n, hn, heads, hc, dh, qb, kbr)
    span = STEPS * qb
    dma = pltpu.SemaphoreType.DMA
    return pl.pallas_call(
        functools.partial(kernel, dims),
        out_shape=(
            jax.ShapeDtypeStruct((kbr, feats), BF16),
            jax.ShapeDtypeStruct((kbr, feats), BF16),
            jax.ShapeDtypeStruct((qb // hn, feats * hn), BF16),
        ),
        in_specs=[pl.BlockSpec(memory_space=pl.ANY)] * 7,
        out_specs=tuple([pl.BlockSpec(memory_space=pl.ANY)] * 3),
        scratch_shapes=[
            pltpu.VMEM((chunks, 2, span, w), BF16),
            pltpu.VMEM((chunks, kbr, w), BF16),
            pltpu.VMEM((chunks, kbr, w), BF16),
            pltpu.VMEM((qb, feats), BF16),
            pltpu.VMEM((heads, qb), F32),
            pltpu.VMEM((1, qb), jnp.int32),
            pltpu.VMEM((STEPS, heads, 2 * qb), F32),
            pltpu.VMEM((heads, span), F32),
            pltpu.VMEM((heads, span), F32),
            pltpu.VMEM((1, span), jnp.int32),
            pltpu.VMEM((chunks, span, w), F32),
            pltpu.VMEM((chunks, span, w), BF16),
            pltpu.VMEM((3, chunks, qb, w), BF16),
            pltpu.VMEM((chunks, qb, w), BF16),
            pltpu.VMEM((chunks, kbr, w), BF16),
            pltpu.VMEM((chunks, kbr, w), BF16),
            pltpu.VMEM((qb // hn, feats * hn), BF16),
            dma((2, chunks)), dma((2, chunks)), dma((3,)),
            dma((3, chunks)), dma((3, chunks)), dma((3,)), dma((3,)),
            dma((3, chunks)), dma((3, chunks)),
            dma((max(hn - 1, 1), chunks)), dma((max(hn - 1, 1), chunks)),
            dma((2, chunks)), dma(()),
        ],
        compiler_params=pltpu.CompilerParams(
            collective_id=0, has_side_effects=True, vmem_limit_bytes=64_500 * 1024
        ),
    )(query, query_offset.reshape(1, qb), attn_out, out_grad, log_norm, keys, values)


def solution(mesh):
    in_specs = (
        P("seq", "head"),
        P("seq"),
        P("seq", "head"),
        P("seq", "head"),
        P("head", "seq"),
        P("seq", "head"),
        P("seq", "head"),
    )
    out_specs = (P("seq", "head"), P("seq", "head"), P(("seq", "head"), None))
    return jax.shard_map(
        per_device, mesh=mesh, in_specs=in_specs, out_specs=out_specs, check_vma=False
    )
```

profile of v0, /device:TPU:8, one launch (start us, length us, event | category | flops | bytes accessed | tf_op | source)
XLA Modules:
  0.0 43.9 jit_solution(9787642331774749274)
XLA Ops:
  0.6 38.8 %shard_map.94 = (bf16[256,2560]{1,0:T(8,128)(2,1)}, bf16[256,2560]{1,0:T(8,128)(2,1)}, bf16[32,5120]{1,0:T(8,128)(2,1)}) custom-call(bf16[64,2560]{1,0:T(8,128)(2,1)} %q_hbm.1, s32[1,64]{1,0:T(1,128)} %bitcast.1, bf16[64,2560]{1,0:T(8,128)(2,1)} %o_hbm.1, bf16[64,2560]{1,0:T(8,128)(2,1)} %do_hbm.1, f32[20,64]{1,0:T(8,128)} %ln_hbm.1, ...), custom_call_target="tpu_custom_call" | custom-call | tf_op jit(solution)/shard_map/pallas_call | solution.py:333
  39.5 0.0 copy-start
  39.5 2.6 %copy.13 = bf16[256,2560]{1,0:T(8,128)(2,1)} copy(bf16[256,2560]{1,0:T(8,128)(2,1)} %get-tuple-element.6) | data formatting | bytes 2621440
  42.0 0.0 copy-done
  42.1 0.0 copy-start.1
  42.1 1.1 %copy.14 = bf16[256,2560]{1,0:T(8,128)(2,1)} copy(bf16[256,2560]{1,0:T(8,128)(2,1)S(1)} %copy-done) | data formatting | bytes 2621440
  43.1 0.1 copy-done.1
  43.2 0.7 %copy.15 = bf16[32,5120]{1,0:T(8,128)(2,1)} copy(bf16[32,5120]{1,0:T(8,128)(2,1)S(1)} %copy-done.1) | data formatting | bytes 655360
Async XLA Ops:
  39.5 2.6 %copy-start = (bf16[256,2560]{1,0:T(8,128)(2,1)S(1)}, bf16[256,2560]{1,0:T(8,128)(2,1)}, u32[]{:S(2)}) copy-start(bf16[256,2560]{1,0:T(8,128)(2,1)} %get-tuple-element.7) | copy-start | bytes 3932164
  42.1 1.2 %copy-start.1 = (bf16[32,5120]{1,0:T(8,128)(2,1)S(1)}, bf16[32,5120]{1,0:T(8,128)(2,1)}, u32[]{:S(2)}) copy-start(bf16[32,5120]{1,0:T(8,128)(2,1)} %get-tuple-element.8) | copy-start | bytes 983044
where the time goes:
time: 44.1 us; the launch traced here: 43.9 us
  Pallas kernels  38.8 us (88%)
  local copies, waits for them, and re-layouts  4.45 us (10%)
  between operations  0.65 us (1%)
    pallas_call x1, Pallas kernels, per_device(): pl.pallas_call(functools.partial(kernel, dims), out_shape=(jax.ShapeDtype...  38.8 us
    unnamed x7, local copies, waits for them, and re-layouts  4.45 us

commit v1 on v0

v1 whole, which is shorter than its diff:
```python
import functools
import math

import jax
import jax.numpy as jnp
from jax import lax
from jax.experimental import pallas as pl
from jax.experimental.pallas import tpu as pltpu
from jax.sharding import PartitionSpec as P

STEPS = 4
HEADS_PER_CHUNK = 2
LAG0 = 1
LAG1 = 1
WAIT0 = 5
RATE0 = 2
LATE = 7
AHEAD = 2
F32 = jnp.float32
BF16 = jnp.bfloat16


def dot(a, b, ca, cb):
    return lax.dot_general(a, b, (((ca,), (cb,)), ((), ())), preferred_element_type=F32)


def kernel(
    dims, q_hbm, off_hbm, o_hbm, do_hbm, ln_hbm, k_hbm, v_hbm,
    kgb, vgb, outb,
    x, via, kb, vb, ob, lnb, offb, st, lse, dlt, offrow, own, part, got, fin,
    load_sem, kv_sem, small_sem, xs, xr, ss, sr, ps, pr, fs, fr,
):
    n, hn, heads, hc, dh, qb, kbr = dims
    chunks = heads // hc
    w = hc * dh
    feats = heads * dh
    rows_out = qb // hn
    scale = 1.0 / math.sqrt(dh)
    me = lax.axis_index("seq")
    hd = lax.axis_index("head")
    k = lax.rem(me, 2)
    partner = me + 1 - 2 * k
    oa = 1 + 2 * k
    oc = 3 - 2 * k
    quad = lax.rem(me, 4)
    q0, q1, q2, q3 = (quad == i for i in range(4))
    odd = k == 1
    lower = me >= 4
    has2 = me + 2 < n
    hasa = me + oa < n
    to2 = me >= 2
    toc = me >= oc

    def rows(o):
        return pl.ds(pl.multiple_of(o * qb, qb), qb)

    def cols(g):
        return pl.ds(pl.multiple_of(g * w, w), w)

    def load_q(g):
        return pltpu.make_async_copy(q_hbm.at[:, cols(g)], x.at[g, 0, pl.ds(0, qb)], load_sem.at[0, g])

    def load_do(g):
        return pltpu.make_async_copy(do_hbm.at[:, cols(g)], x.at[g, 1, pl.ds(0, qb)], load_sem.at[1, g])

    def load_k(g):
        return pltpu.make_async_copy(k_hbm.at[:, cols(g)], kb.at[g], kv_sem.at[0, g])

    def load_v(g):
        return pltpu.make_async_copy(v_hbm.at[:, cols(g)], vb.at[g], kv_sem.at[1, g])

    load_o = pltpu.make_async_copy(o_hbm, ob, small_sem.at[0])
    load_ln = pltpu.make_async_copy(ln_hbm, lnb, small_sem.at[1])
    load_off = pltpu.make_async_copy(off_hbm, offb, small_sem.at[2])

    def remote(src, dst, send, recv, target):
        return pltpu.make_async_remote_copy(
            src_ref=src, dst_ref=dst, send_sem=send, recv_sem=recv,
            device_id={"seq": target}, device_id_type=pl.DeviceIdType.MESH,
        )

    def mine(g):
        return x.at[g, :, pl.ds(0, qb)]

    def slot(g, o):
        return x.at[g, :, rows(o)]

    def x_two(g):
        return remote(mine(g), slot(g, 2), xs.at[0, g], xr.at[0, g], me - 2)

    def x_chip(g):
        return remote(mine(g), slot(g, 1), xs.at[1, g], xr.at[1, g], me - 1)

    def x_three(g):
        return remote(mine(g), slot(g, 3), xs.at[1, g], xr.at[1, g], me - 3)

    def x_side(g):
        return remote(mine(g), via.at[g], xs.at[0, g], xr.at[3, g], me + 3)

    def via_down(g):
        return remote(via.at[g], slot(g, 2), xs.at[3, g], xr.at[0, g], me - 5)

    def x_relay(g):
        return remote(slot(g, 2), slot(g, oa), xs.at[2, g], xr.at[2, g], partner)

    def st_send(o):
        return remote(st.at[0], st.at[o], ss.at[o - 1], sr.at[o - 1], me - o)

    def p_partner(g):
        return remote(part.at[g, rows(oc)], got.at[0, g], ps.at[0, g], pr.at[0, g], partner)

    def p_ahead(g):
        return remote(part.at[g, rows(oa)], got.at[1, g], ps.at[1, g], pr.at[1, g], me + oa)

    def p_two(g):
        return remote(part.at[g, rows(2)], got.at[2, g], ps.at[2, g], pr.at[2, g], me + 2)

    def f_send(g, d):
        peer = lax.rem(hd + d, hn)
        return pltpu.make_async_remote_copy(
            src_ref=fin.at[g, pl.ds(pl.multiple_of(peer * rows_out, rows_out), rows_out)],
            dst_ref=outb.at[:, pl.ds(pl.multiple_of(hd * feats + g * w, w), w)],
            send_sem=fs.at[d - 1, g], recv_sem=fr.at[d - 1, g],
            device_id={"head": peer}, device_id_type=pl.DeviceIdType.MESH,
        )

    @pl.loop(0, chunks)
    def _(g):
        load_do(g).start()
        load_q(g).start()

    load_o.start()
    load_ln.start()
    load_off.start()

    barrier = pltpu.get_barrier_semaphore()

    def greet(cond, target):
        @pl.when(cond)
        def _():
            pl.semaphore_signal(barrier, inc=1, device_id={"seq": target}, device_id_type=pl.DeviceIdType.MESH)

        return cond.astype(jnp.int32)

    peers = hn - 1
    for d in (1, 2, 3, 5):
        peers = peers + greet(me >= d, me - d) + greet(me + d < n, me + d)
    for d in range(1, hn):
        pl.semaphore_signal(
            barrier, inc=1, device_id={"head": lax.rem(hd + d, hn)}, device_id_type=pl.DeviceIdType.MESH
        )

    load_o.wait()
    load_ln.wait()

    @pl.loop(0, chunks)
    def _(g):
        load_q(g).wait()
        load_do(g).wait()

    st[0, :, 0:qb] = lnb[...]
    eye = lax.broadcasted_iota(jnp.int32, (qb, qb), 0) == lax.broadcasted_iota(jnp.int32, (qb, qb), 1)
    for h in range(heads):
        oh = ob[:, h * dh:(h + 1) * dh]
        doh = x[h // hc, 1, 0:qb, h % hc * dh:(h % hc + 1) * dh]
        t = dot(oh, doh, 1, 1)
        st[0, h:h + 1, qb:2 * qb] = jnp.sum(jnp.where(eye, t, 0.0), axis=0, keepdims=True)

    pl.semaphore_wait(barrier, peers)

    def send_x(g):
        pl.when(q2 | q3 | (q1 & lower))(lambda: x_two(g).start())
        pl.when(q0 & lower)(lambda: x_side(g).start())
        pl.when(odd)(lambda: x_chip(g).start())
        pl.when((q0 | q2) & lower)(lambda: x_three(g).start())

    send_x(0)

    for o in range(1, STEPS):
        pl.when(me >= o)(lambda o=o: st_send(o).start())

    @pl.loop(1, chunks)
    def _(g):
        send_x(g)

    @pl.loop(0, chunks)
    def _(g):
        load_k(g).start()
        load_v(g).start()

    for o in range(1, STEPS):

        @pl.when(me + o >= n)
        def _(o=o):
            @pl.loop(0, chunks)
            def _(g):
                for i in range(2):
                    x[g, i, rows(o), :] = jnp.zeros((qb, w), BF16)

            st[o] = jnp.zeros_like(st[o])

    load_off.wait()
    offrow[...] = jnp.full(offrow.shape, kbr, jnp.int32)
    offrow[:, 0:qb] = offb[...]

    def forward(g):
        @pl.when(q3 & lower)
        def _():
            x_side(g).wait_recv()
            via_down(g).start()

    def relay(g):
        @pl.when(has2)
        def _():
            x_two(g).wait_recv()
            x_relay(g).start()

    def compute(g):
        @pl.when(hasa)
        def _():
            x_chip(g).wait_recv()

        pl.when(has2)(lambda: x_relay(g).wait_recv())
        load_k(g).wait()
        load_v(g).wait()
        allowed = lax.broadcasted_iota(jnp.int32, (kbr, STEPS * qb), 0) <= offrow[...]
        for h in range(hc):
            c = slice(h * dh, (h + 1) * dh)
            qh = x[g, 0, :, c]
            doh = x[g, 1, :, c]
            kh = kb[g, :, c]
            vh = vb[g, :, c]
            row = pl.ds(g * hc + h, 1)
            s = dot(kh, qh, 1, 1) * scale - lse[row, :]
            p = jnp.where(allowed, jnp.exp(s), 0.0)
            dp = dot(vh, doh, 1, 1)
            ds = (p * (dp - dlt[row, :]) * scale).astype(BF16)
            out = pl.ds(pl.multiple_of(g * w + h * dh, dh), dh)
            vgb[:, out] = dot(p.astype(BF16), doh, 1, 0).astype(BF16)
            kgb[:, out] = dot(ds, qh, 1, 0).astype(BF16)
            dq = dot(ds, kh, 0, 0)
            own[g, :, c] = dq
            part[g, :, c] = dq.astype(BF16)
        pl.when(has2)(lambda: p_partner(g).start())
        pl.when(hasa)(lambda: p_ahead(g).start())

    def combine(g):
        @pl.when(has2)
        def _():
            p_partner(g).wait_recv()
            both = own[g, 2 * qb:3 * qb, :] + got[0, g].astype(F32)
            part[g, 2 * qb:3 * qb, :] = both.astype(BF16)
            p_two(g).start()

    def finish(g):
        @pl.when(to2)
        def _():
            p_two(g).wait_recv()
            own[g, 0:qb, :] = own[g, 0:qb, :] + got[2, g].astype(F32)

        @pl.when(toc)
        def _():
            p_ahead(g).wait_recv()
            own[g, 0:qb, :] = own[g, 0:qb, :] + got[1, g].astype(F32)

        fin[g] = own[g, 0:qb, :].astype(BF16)
        for d in range(1, hn):
            f_send(g, d).start()
        outb[:, pl.ds(pl.multiple_of(hd * feats + g * w, w), w)] = fin[
            g, pl.ds(pl.multiple_of(hd * rows_out, rows_out), rows_out), :
        ]

    for g in range(min(AHEAD, chunks)):
        forward(g)
    relay(0)

    for o in range(1, STEPS):
        pl.when(me + o < n)(lambda o=o: st_send(o).wait_recv())
    for o in range(STEPS):
        lse[:, o * qb:(o + 1) * qb] = st[o, :, 0:qb]
        dlt[:, o * qb:(o + 1) * qb] = st[o, :, qb:2 * qb]

    def sent(t):
        below = jnp.clip((t - WAIT0) * RATE0, 0, t - LAG0)
        return jnp.clip(jnp.where((quad < 2) & (me + 4 < n), below, t - LAG1), 0, chunks)

    def done(t):
        return jnp.clip(t - jnp.where(me < 2, 1, LATE), 0, chunks)

    @pl.loop(1, chunks + 1)
    def _(t):
        pl.when(t + AHEAD - 1 < chunks)(lambda: forward(t + AHEAD - 1))
        pl.when(t < chunks)(lambda: relay(t))
        compute(t - 1)

        @pl.loop(sent(t - 1), sent(t))
        def _(g):
            combine(g)

        @pl.loop(done(t - 1), done(t))
        def _(g):
            finish(g)

    @pl.loop(sent(chunks), chunks)
    def _(g):
        combine(g)

    @pl.loop(done(chunks), chunks)
    def _(g):
        finish(g)

    @pl.loop(0, chunks)
    def _(g):
        pl.when(q2 | q3 | lower)(lambda: x_two(g).wait_send())
        pl.when(odd | lower)(lambda: x_chip(g).wait_send())
        pl.when(q3 & lower)(lambda: via_down(g).wait_send())

        @pl.when(has2)
        def _():
            x_relay(g).wait_send()
            p_partner(g).wait_send()
            p_two(g).wait_send()

        pl.when(hasa)(lambda: p_ahead(g).wait_send())

    for o in range(1, STEPS):
        pl.when(me >= o)(lambda o=o: st_send(o).wait_send())

    @pl.loop(0, chunks)
    def _(g):
        for d in range(1, hn):
            f_send(g, d).wait()


def write_out(kgb, vgb, outb, kg_hbm, vg_hbm, qg_hbm, sem):
    copies = [
        pltpu.make_async_copy(src, dst, sem.at[i])
        for i, (src, dst) in enumerate(((kgb, kg_hbm), (vgb, vg_hbm), (outb, qg_hbm)))
    ]
    for copy in copies:
        copy.start()
    for copy in copies:
        copy.wait()


def per_device(query, query_offset, attn_out, out_grad, log_norm, keys, values):
    n = lax.axis_size("seq")
    hn = lax.axis_size("head")
    heads = log_norm.shape[0]
    qb, feats = query.shape
    kbr = keys.shape[0]
    dh = feats // heads
    hc = HEADS_PER_CHUNK
    while heads % hc:
        hc -= 1
    chunks = heads // hc
    w = hc * dh
    dims = (n, hn, heads, hc, dh, qb, kbr)
    span = STEPS * qb
    dma = pltpu.SemaphoreType.DMA
    args = (query, query_offset.reshape(1, qb), attn_out, out_grad, log_norm, keys, values)
    outs = (
        jax.ShapeDtypeStruct((kbr, feats), BF16),
        jax.ShapeDtypeStruct((kbr, feats), BF16),
        jax.ShapeDtypeStruct((qb // hn, feats * hn), BF16),
    )
    grads = pl.pallas_call(
        functools.partial(kernel, dims),
        out_shape=tuple(pltpu.VMEM(o.shape, o.dtype) for o in outs),
        in_specs=[pl.BlockSpec(memory_space=pl.ANY)] * 7,
        out_specs=tuple([pl.BlockSpec(memory_space=pltpu.VMEM)] * 3),
        scratch_shapes=[
            pltpu.VMEM((chunks, 2, span, w), BF16),
            pltpu.VMEM((chunks, 2, qb, w), BF16),
            pltpu.VMEM((chunks, kbr, w), BF16),
            pltpu.VMEM((chunks, kbr, w), BF16),
            pltpu.VMEM((qb, feats), BF16),
            pltpu.VMEM((heads, qb), F32),
            pltpu.VMEM((1, qb), jnp.int32),
            pltpu.VMEM((STEPS, heads, 2 * qb), F32),
            pltpu.VMEM((heads, span), F32),
            pltpu.VMEM((heads, span), F32),
            pltpu.VMEM((1, span), jnp.int32),
            pltpu.VMEM((chunks, span, w), F32),
            pltpu.VMEM((chunks, span, w), BF16),
            pltpu.VMEM((3, chunks, qb, w), BF16),
            pltpu.VMEM((chunks, qb, w), BF16),
            dma((2, chunks)), dma((2, chunks)), dma((3,)),
            dma((4, chunks)), dma((4, chunks)), dma((3,)), dma((3,)),
            dma((3, chunks)), dma((3, chunks)),
            dma((max(hn - 1, 1), chunks)), dma((max(hn - 1, 1), chunks)),
        ],
        compiler_params=pltpu.CompilerParams(
            collective_id=0, has_side_effects=True, vmem_limit_bytes=40 * 1024 * 1024
        ),
    )(*[pltpu.with_memory_space_constraint(a, pltpu.HBM) for a in args])
    return pl.pallas_call(
        write_out,
        out_shape=outs,
        in_specs=[pl.BlockSpec(memory_space=pltpu.VMEM)] * 3,
        out_specs=tuple([pl.BlockSpec(memory_space=pl.ANY)] * 3),
        scratch_shapes=[dma((3,))],
        compiler_params=pltpu.CompilerParams(vmem_limit_bytes=16 * 1024 * 1024),
    )(*grads)


def solution(mesh):
    in_specs = (
        P("seq", "head"),
        P("seq"),
        P("seq", "head"),
        P("seq", "head"),
        P("head", "seq"),
        P("seq", "head"),
        P("seq", "head"),
    )
    out_specs = (P("seq", "head"), P("seq", "head"), P(("seq", "head"), None))
    return jax.shard_map(
        per_device, mesh=mesh, in_specs=in_specs, out_specs=out_specs, check_vma=False
    )
```

time: 44.1 us -> 36.5 us (0.83)
  local copies, waits for them, and re-layouts: 4.45 us -> 0 us
  Pallas kernels: 38.8 us -> 35.7 us
    unnamed x7 -> x0, local copies, waits for them, and re-layouts: 4.45 us -> none
    pallas_call x1 -> x2, Pallas kernels: 38.8 us -> 35.7 us  [the longest x1 34.1 us: per_device(): pl.pallas_call(functools.partial(kernel, dims), out_shape=tuple((pltpu.VM...]
where the time goes in v1:
time: 36.5 us; the launch traced here: 36.4 us
  Pallas kernels  35.7 us (98%)
  between operations  0.64 us (2%)
    pallas_call x1, Pallas kernels, per_device(): pl.pallas_call(functools.partial(kernel, dims), out_shape=tuple((pltpu.VM...  34.1 us
    pallas_call x1, Pallas kernels, per_device(): pl.pallas_call(write_out, out_shape=outs, in_specs=[pl.BlockSpec(memory_s...  1.62 us

profile of v1, /device:TPU:8, one launch (start us, length us, event | category | flops | bytes accessed | tf_op | source)
XLA Modules:
  0.0 36.4 jit_solution(14544123039886819576)
XLA Ops:
  0.6 34.1 %shard_map.94 = (bf16[256,2560]{1,0:T(8,128)(2,1)S(1)}, bf16[256,2560]{1,0:T(8,128)(2,1)S(1)}, bf16[32,5120]{1,0:T(8,128)(2,1)S(1)}) custom-call(bf16[64,2560]{1,0:T(8,128)(2,1)} %q_hbm.1, s32[1,64]{1,0:T(1,128)} %bitcast.1, bf16[64,2560]{1,0:T(8,128)(2,1)} %o_hbm.1, bf16[64,2560]{1,0:T(8,128)(2,1)} %do_hbm.1, f32[20,64]{1,0:T(8,128)} %ln_hbm.1, ...), custom_call_target="tpu_custom_call" | custom-call | tf_op jit(solution)/shard_map/pallas_call | solution.py:367
  34.8 1.6 %shard_map.95 = (bf16[256,2560]{1,0:T(8,128)(2,1)}, bf16[256,2560]{1,0:T(8,128)(2,1)}, bf16[32,5120]{1,0:T(8,128)(2,1)}) custom-call(bf16[256,2560]{1,0:T(8,128)(2,1)S(1)} %get-tuple-element.6.kgb, bf16[256,2560]{1,0:T(8,128)(2,1)S(1)} %get-tuple-element.7.vgb, bf16[32,5120]{1,0:T(8,128)(2,1)S(1)} %get-tuple-element.8.outb), custom_call_target="tpu_custom_call" | custom-call | tf_op jit(solution)/shard_map/pallas_call | solution.py:397

commit v2 on v1

--- a/solution.py
+++ b/solution.py
@@ -14,8 +14,9 @@
 LAG1 = 1
 WAIT0 = 5
 RATE0 = 2
-LATE = 7
-AHEAD = 2
+FROM = 2
+UPTO = 8
+AHEAD = 3
 F32 = jnp.float32
 BF16 = jnp.bfloat16
 
@@ -27,8 +28,8 @@
 def kernel(
     dims, q_hbm, off_hbm, o_hbm, do_hbm, ln_hbm, k_hbm, v_hbm,
     kgb, vgb, outb,
-    x, via, kb, vb, ob, lnb, offb, st, lse, dlt, offrow, own, part, got, fin,
-    load_sem, kv_sem, small_sem, xs, xr, ss, sr, ps, pr, fs, fr,
+    x, via, kb, vb, ob, lnb, offb, st, lse, dlt, offrow, own, part, got, mate,
+    load_sem, kv_sem, small_sem, xs, xr, ss, sr, ps, pr, rsnd, rrcv,
 ):
     n, hn, heads, hc, dh, qb, kbr = dims
     chunks = heads // hc
@@ -100,6 +101,9 @@
     def via_down(g):
         return remote(via.at[g], slot(g, 2), xs.at[3, g], xr.at[0, g], me - 5)
 
+    def relayed(g):
+        return (g >= chunks * FROM // 10) & (g < chunks * UPTO // 10)
+
     def x_relay(g):
         return remote(slot(g, 2), slot(g, oa), xs.at[2, g], xr.at[2, g], partner)
 
@@ -107,22 +111,30 @@
         return remote(st.at[0], st.at[o], ss.at[o - 1], sr.at[o - 1], me - o)
 
     def p_partner(g):
-        return remote(part.at[g, rows(oc)], got.at[0, g], ps.at[0, g], pr.at[0, g], partner)
-
-    def p_ahead(g):
-        return remote(part.at[g, rows(oa)], got.at[1, g], ps.at[1, g], pr.at[1, g], me + oa)
-
-    def p_two(g):
-        return remote(part.at[g, rows(2)], got.at[2, g], ps.at[2, g], pr.at[2, g], me + 2)
-
-    def f_send(g, d):
+        return remote(part.at[g, rows(oc)], got.at[g], ps.at[g], pr.at[g], partner)
+
+    def piece(hs):
+        return pl.multiple_of(hs * rows_out, rows_out)
+
+    def back(kind, g, d, ahead, o):
         peer = lax.rem(hd + d, hn)
         return pltpu.make_async_remote_copy(
-            src_ref=fin.at[g, pl.ds(pl.multiple_of(peer * rows_out, rows_out), rows_out)],
-            dst_ref=outb.at[:, pl.ds(pl.multiple_of(hd * feats + g * w, w), w)],
-            send_sem=fs.at[d - 1, g], recv_sem=fr.at[d - 1, g],
-            device_id={"head": peer}, device_id_type=pl.DeviceIdType.MESH,
+            src_ref=part.at[g, pl.ds(pl.multiple_of(o * qb, qb) + piece(peer), rows_out)],
+            dst_ref=mate.at[kind, hd, g], send_sem=rsnd.at[kind, d, g], recv_sem=rrcv.at[kind, hd, g],
+            device_id={"seq": me + ahead, "head": peer}, device_id_type=pl.DeviceIdType.MESH,
         )
+
+    def p_own(g, d):
+        return back(0, g, d, 0, 0)
+
+    def p_ahead(g, d):
+        return back(1, g, d, oa, oa)
+
+    def p_two(g, d):
+        return back(2, g, d, 2, 2)
+
+    def arrived(kind, g, hs):
+        return pltpu.make_async_copy(mate.at[kind, hs, g], mate.at[kind, hs, g], rrcv.at[kind, hs, g])
 
     @pl.loop(0, chunks)
     def _(g):
@@ -135,20 +147,23 @@
 
     barrier = pltpu.get_barrier_semaphore()
 
-    def greet(cond, target):
+    def greet(cond, ahead, d=0):
         @pl.when(cond)
         def _():
-            pl.semaphore_signal(barrier, inc=1, device_id={"seq": target}, device_id_type=pl.DeviceIdType.MESH)
+            pl.semaphore_signal(
+                barrier, inc=1, device_id={"seq": me + ahead, "head": lax.rem(hd + d, hn)},
+                device_id_type=pl.DeviceIdType.MESH,
+            )
 
         return cond.astype(jnp.int32)
 
-    peers = hn - 1
-    for d in (1, 2, 3, 5):
-        peers = peers + greet(me >= d, me - d) + greet(me + d < n, me + d)
+    peers = 0
+    for o in range(1, STEPS):
+        peers = peers + greet(me >= o, -o) + greet(me + o < n, o)
+    peers = peers + greet(q3 & lower, -5) + greet(q2 & (me + 5 < n), 5)
     for d in range(1, hn):
-        pl.semaphore_signal(
-            barrier, inc=1, device_id={"head": lax.rem(hd + d, hn)}, device_id_type=pl.DeviceIdType.MESH
-        )
+        peers = peers + greet(me >= 0, 0, d)
+        peers = peers + greet(to2, -2, d) + greet(has2, 2, d) + greet(toc, -oc, d) + greet(hasa, oa, d)
 
     load_o.wait()
     load_ln.wait()
@@ -169,8 +184,8 @@
     pl.semaphore_wait(barrier, peers)
 
     def send_x(g):
-        pl.when(q2 | q3 | (q1 & lower))(lambda: x_two(g).start())
-        pl.when(q0 & lower)(lambda: x_side(g).start())
+        pl.when(q2 | q3 | (lower & (q1 | (q0 & jnp.logical_not(relayed(g))))))(lambda: x_two(g).start())
+        pl.when(q0 & lower & relayed(g))(lambda: x_side(g).start())
         pl.when(odd)(lambda: x_chip(g).start())
         pl.when((q0 | q2) & lower)(lambda: x_three(g).start())
 
@@ -204,7 +219,7 @@
     offrow[:, 0:qb] = offb[...]
 
     def forward(g):
-        @pl.when(q3 & lower)
+        @pl.when(q3 & lower & relayed(g))
         def _():
             x_side(g).wait_recv()
             via_down(g).start()
@@ -242,33 +257,41 @@
             own[g, :, c] = dq
             part[g, :, c] = dq.astype(BF16)
         pl.when(has2)(lambda: p_partner(g).start())
-        pl.when(hasa)(lambda: p_ahead(g).start())
+        for d in range(hn):
+            pl.when(hasa)(lambda d=d: p_ahead(g, d).start())
+            if d:
+                p_own(g, d).start()
 
     def combine(g):
         @pl.when(has2)
         def _():
             p_partner(g).wait_recv()
-            both = own[g, 2 * qb:3 * qb, :] + got[0, g].astype(F32)
+            both = own[g, 2 * qb:3 * qb, :] + got[g].astype(F32)
             part[g, 2 * qb:3 * qb, :] = both.astype(BF16)
-            p_two(g).start()
+            for d in range(hn):
+                p_two(g, d).start()
 
     def finish(g):
-        @pl.when(to2)
-        def _():
-            p_two(g).wait_recv()
-            own[g, 0:qb, :] = own[g, 0:qb, :] + got[2, g].astype(F32)
-
-        @pl.when(toc)
-        def _():
-            p_ahead(g).wait_recv()
-            own[g, 0:qb, :] = own[g, 0:qb, :] + got[1, g].astype(F32)
-
-        fin[g] = own[g, 0:qb, :].astype(BF16)
-        for d in range(1, hn):
-            f_send(g, d).start()
-        outb[:, pl.ds(pl.multiple_of(hd * feats + g * w, w), w)] = fin[
-            g, pl.ds(pl.multiple_of(hd * rows_out, rows_out), rows_out), :
-        ]
+        for d in range(hn):
+            hs = lax.rem(hd + d, hn)
+            if d:
+                arrived(0, g, hs).wait()
+                total = mate[0, hs, g].astype(F32)
+            else:
+                total = own[g, pl.ds(piece(hd), rows_out), :]
+            here = pl.ds(pl.multiple_of(hs * feats + g * w, w), w)
+
+            @pl.when(toc)
+            def _():
+                arrived(1, g, hs).wait()
+
+            @pl.when(to2)
+            def _():
+                arrived(2, g, hs).wait()
+
+            total = total + jnp.where(toc, mate[1, hs, g].astype(F32), 0.0)
+            total = total + jnp.where(to2, mate[2, hs, g].astype(F32), 0.0)
+            outb[:, here] = total.astype(BF16)
 
     for g in range(min(AHEAD, chunks)):
         forward(g)
@@ -284,9 +307,6 @@
         below = jnp.clip((t - WAIT0) * RATE0, 0, t - LAG0)
         return jnp.clip(jnp.where((quad < 2) & (me + 4 < n), below, t - LAG1), 0, chunks)
 
-    def done(t):
-        return jnp.clip(t - jnp.where(me < 2, 1, LATE), 0, chunks)
-
     @pl.loop(1, chunks + 1)
     def _(t):
         pl.when(t + AHEAD - 1 < chunks)(lambda: forward(t + AHEAD - 1))
@@ -297,39 +317,33 @@
         def _(g):
             combine(g)
 
-        @pl.loop(done(t - 1), done(t))
-        def _(g):
-            finish(g)
-
     @pl.loop(sent(chunks), chunks)
     def _(g):
         combine(g)
-
-    @pl.loop(done(chunks), chunks)
-    def _(g):
-        finish(g)
 
     @pl.loop(0, chunks)
     def _(g):
         pl.when(q2 | q3 | lower)(lambda: x_two(g).wait_send())
         pl.when(odd | lower)(lambda: x_chip(g).wait_send())
-        pl.when(q3 & lower)(lambda: via_down(g).wait_send())
+        pl.when(q3 & lower & relayed(g))(lambda: via_down(g).wait_send())
 
         @pl.when(has2)
         def _():
             x_relay(g).wait_send()
             p_partner(g).wait_send()
-            p_two(g).wait_send()
-
-        pl.when(hasa)(lambda: p_ahead(g).wait_send())
+
+        for d in range(1, hn):
+            p_own(g, d).wait_send()
 
     for o in range(1, STEPS):
         pl.when(me >= o)(lambda o=o: st_send(o).wait_send())
 
     @pl.loop(0, chunks)
     def _(g):
-        for d in range(1, hn):
-            f_send(g, d).wait()
+        finish(g)
+        for d in range(hn):
+            pl.when(hasa)(lambda d=d: p_ahead(g, d).wait_send())
+            pl.when(has2)(lambda d=d: p_two(g, d).wait_send())
 
 
 def write_out(kgb, vgb, outb, kg_hbm, vg_hbm, qg_hbm, sem):
@@ -383,12 +397,12 @@
             pltpu.VMEM((1, span), jnp.int32),
             pltpu.VMEM((chunks, span, w), F32),
             pltpu.VMEM((chunks, span, w), BF16),
-            pltpu.VMEM((3, chunks, qb, w), BF16),
             pltpu.VMEM((chunks, qb, w), BF16),
+            pltpu.VMEM((3, hn, chunks, qb // hn, w), BF16),
             dma((2, chunks)), dma((2, chunks)), dma((3,)),
             dma((4, chunks)), dma((4, chunks)), dma((3,)), dma((3,)),
-            dma((3, chunks)), dma((3, chunks)),
-            dma((max(hn - 1, 1), chunks)), dma((max(hn - 1, 1), chunks)),
+            dma((chunks,)), dma((chunks,)),
+            dma((3, hn, chunks)), dma((3, hn, chunks)),
         ],
         compiler_params=pltpu.CompilerParams(
             collective_id=0, has_side_effects=True, vmem_limit_bytes=40 * 1024 * 1024

time: 36.5 us -> 33.5 us (0.918)
  Pallas kernels: 35.7 us -> 32.7 us
    pallas_call x1, Pallas kernels: 34.1 us -> 31.1 us  [per_device(): pl.pallas_call(functools.partial(kernel, dims), out_shape=tuple((pltpu.VM...]
where the time goes in v2:
time: 33.5 us; the launch traced here: 33.4 us
  Pallas kernels  32.7 us (98%)
  between operations  0.64 us (2%)
    pallas_call x1, Pallas kernels, per_device(): pl.pallas_call(functools.partial(kernel, dims), out_shape=tuple((pltpu.VM...  31.1 us
    pallas_call x1, Pallas kernels, per_device(): pl.pallas_call(write_out, out_shape=outs, in_specs=[pl.BlockSpec(memory_s...  1.62 us

profile of v2, /device:TPU:8, one launch (start us, length us, event | category | flops | bytes accessed | tf_op | source)
XLA Modules:
  0.0 33.4 jit_solution(16702847658729238586)
XLA Ops:
  0.6 31.1 %shard_map.94 = (bf16[256,2560]{1,0:T(8,128)(2,1)S(1)}, bf16[256,2560]{1,0:T(8,128)(2,1)S(1)}, bf16[32,5120]{1,0:T(8,128)(2,1)S(1)}) custom-call(bf16[64,2560]{1,0:T(8,128)(2,1)} %q_hbm.1, s32[1,64]{1,0:T(1,128)} %bitcast.1, bf16[64,2560]{1,0:T(8,128)(2,1)} %o_hbm.1, bf16[64,2560]{1,0:T(8,128)(2,1)} %do_hbm.1, f32[20,64]{1,0:T(8,128)} %ln_hbm.1, ...), custom_call_target="tpu_custom_call" | custom-call | tf_op jit(solution)/shard_map/pallas_call | solution.py:381
  31.7 1.6 %shard_map.95 = (bf16[256,2560]{1,0:T(8,128)(2,1)}, bf16[256,2560]{1,0:T(8,128)(2,1)}, bf16[32,5120]{1,0:T(8,128)(2,1)}) custom-call(bf16[256,2560]{1,0:T(8,128)(2,1)S(1)} %get-tuple-element.6.kgb, bf16[256,2560]{1,0:T(8,128)(2,1)S(1)} %get-tuple-element.7.vgb, bf16[32,5120]{1,0:T(8,128)(2,1)S(1)} %get-tuple-element.8.outb), custom_call_target="tpu_custom_call" | custom-call | tf_op jit(solution)/shard_map/pallas_call | solution.py:411

commit v3 on v2

--- a/solution.py
+++ b/solution.py
@@ -12,6 +12,8 @@
 HEADS_PER_CHUNK = 2
 LAG0 = 1
 LAG1 = 1
+WAIT1 = 0
+RATE1 = 9
 WAIT0 = 5
 RATE0 = 2
 FROM = 2
@@ -29,7 +31,7 @@
     dims, q_hbm, off_hbm, o_hbm, do_hbm, ln_hbm, k_hbm, v_hbm,
     kgb, vgb, outb,
     x, via, kb, vb, ob, lnb, offb, st, lse, dlt, offrow, own, part, got, mate,
-    load_sem, kv_sem, small_sem, xs, xr, ss, sr, ps, pr, rsnd, rrcv,
+    small_sem, xs, xr, ss, sr, ps, pr, rsnd, rrcv, ready,
 ):
     n, hn, heads, hc, dh, qb, kbr = dims
     chunks = heads // hc
@@ -52,6 +54,9 @@
     to2 = me >= 2
     toc = me >= oc
 
+    def drain(ref, sem):
+        pltpu.make_async_copy(ref, ref, sem).wait()
+
     def rows(o):
         return pl.ds(pl.multiple_of(o * qb, qb), qb)
 
@@ -59,17 +64,13 @@
         return pl.ds(pl.multiple_of(g * w, w), w)
 
     def load_q(g):
-        return pltpu.make_async_copy(q_hbm.at[:, cols(g)], x.at[g, 0, pl.ds(0, qb)], load_sem.at[0, g])
+        return pltpu.make_async_copy(q_hbm.at[:, cols(g)], x.at[g, 0, pl.ds(0, qb)], small_sem.at[3])
 
     def load_do(g):
-        return pltpu.make_async_copy(do_hbm.at[:, cols(g)], x.at[g, 1, pl.ds(0, qb)], load_sem.at[1, g])
-
-    def load_k(g):
-        return pltpu.make_async_copy(k_hbm.at[:, cols(g)], kb.at[g], kv_sem.at[0, g])
-
-    def load_v(g):
-        return pltpu.make_async_copy(v_hbm.at[:, cols(g)], vb.at[g], kv_sem.at[1, g])
-
+        return pltpu.make_async_copy(do_hbm.at[:, cols(g)], x.at[g, 1, pl.ds(0, qb)], small_sem.at[3])
+
+    load_k = pltpu.make_async_copy(k_hbm, kb, small_sem.at[4])
+    load_v = pltpu.make_async_copy(v_hbm, vb, small_sem.at[5])
     load_o = pltpu.make_async_copy(o_hbm, ob, small_sem.at[0])
     load_ln = pltpu.make_async_copy(ln_hbm, lnb, small_sem.at[1])
     load_off = pltpu.make_async_copy(off_hbm, offb, small_sem.at[2])
@@ -87,31 +88,34 @@
         return x.at[g, :, rows(o)]
 
     def x_two(g):
-        return remote(mine(g), slot(g, 2), xs.at[0, g], xr.at[0, g], me - 2)
+        return remote(mine(g), slot(g, 2), xs.at[0], xr.at[0, g], me - 2)
 
     def x_chip(g):
-        return remote(mine(g), slot(g, 1), xs.at[1, g], xr.at[1, g], me - 1)
+        return remote(mine(g), slot(g, 1), xs.at[1], xr.at[1, g], me - 1)
 
     def x_three(g):
-        return remote(mine(g), slot(g, 3), xs.at[1, g], xr.at[1, g], me - 3)
+        return remote(mine(g), slot(g, 3), xs.at[1], xr.at[1, g], me - 3)
 
     def x_side(g):
-        return remote(mine(g), via.at[g], xs.at[0, g], xr.at[3, g], me + 3)
+        return remote(mine(g), via.at[g], xs.at[0], xr.at[3, g], me + 3)
 
     def via_down(g):
-        return remote(via.at[g], slot(g, 2), xs.at[3, g], xr.at[0, g], me - 5)
+        return remote(via.at[g], slot(g, 2), xs.at[3], xr.at[0, g], me - 5)
+
+    start = chunks * FROM // 10
+    upto = chunks * UPTO // 10
 
     def relayed(g):
-        return (g >= chunks * FROM // 10) & (g < chunks * UPTO // 10)
+        return (g >= start) & (g < upto)
 
     def x_relay(g):
-        return remote(slot(g, 2), slot(g, oa), xs.at[2, g], xr.at[2, g], partner)
+        return remote(slot(g, 2), slot(g, oa), xs.at[2], xr.at[2, g], partner)
 
     def st_send(o):
         return remote(st.at[0], st.at[o], ss.at[o - 1], sr.at[o - 1], me - o)
 
     def p_partner(g):
-        return remote(part.at[g, rows(oc)], got.at[g], ps.at[g], pr.at[g], partner)
+        return remote(part.at[g, rows(oc)], got.at[g], ps, pr.at[g], partner)
 
     def piece(hs):
         return pl.multiple_of(hs * rows_out, rows_out)
@@ -120,7 +124,7 @@
         peer = lax.rem(hd + d, hn)
         return pltpu.make_async_remote_copy(
             src_ref=part.at[g, pl.ds(pl.multiple_of(o * qb, qb) + piece(peer), rows_out)],
-            dst_ref=mate.at[kind, hd, g], send_sem=rsnd.at[kind, d, g], recv_sem=rrcv.at[kind, hd, g],
+            dst_ref=mate.at[kind, hd, g], send_sem=rsnd.at[kind, d], recv_sem=rrcv.at[order(kind, g), hd],
             device_id={"seq": me + ahead, "head": peer}, device_id_type=pl.DeviceIdType.MESH,
         )
 
@@ -133,17 +137,10 @@
     def p_two(g, d):
         return back(2, g, d, 2, 2)
 
-    def arrived(kind, g, hs):
-        return pltpu.make_async_copy(mate.at[kind, hs, g], mate.at[kind, hs, g], rrcv.at[kind, hs, g])
-
-    @pl.loop(0, chunks)
-    def _(g):
-        load_do(g).start()
-        load_q(g).start()
-
-    load_o.start()
-    load_ln.start()
-    load_off.start()
+    bulk = max(chunks - 2, 0)
+
+    def order(kind, g):
+        return kind + jnp.maximum(g - bulk + 1, 0) if kind == 2 else kind
 
     barrier = pltpu.get_barrier_semaphore()
 
@@ -163,15 +160,20 @@
     peers = peers + greet(q3 & lower, -5) + greet(q2 & (me + 5 < n), 5)
     for d in range(1, hn):
         peers = peers + greet(me >= 0, 0, d)
-        peers = peers + greet(to2, -2, d) + greet(has2, 2, d) + greet(toc, -oc, d) + greet(hasa, oa, d)
+
+    @pl.loop(0, chunks)
+    def _(g):
+        load_do(g).start()
+        load_q(g).start()
+
+    load_o.start()
+    load_ln.start()
+    load_off.start()
 
     load_o.wait()
     load_ln.wait()
 
-    @pl.loop(0, chunks)
-    def _(g):
-        load_q(g).wait()
-        load_do(g).wait()
+    drain(x.at[:, :, pl.ds(0, qb)], small_sem.at[3])
 
     st[0, :, 0:qb] = lnb[...]
     eye = lax.broadcasted_iota(jnp.int32, (qb, qb), 0) == lax.broadcasted_iota(jnp.int32, (qb, qb), 1)
@@ -182,6 +184,10 @@
         st[0, h:h + 1, qb:2 * qb] = jnp.sum(jnp.where(eye, t, 0.0), axis=0, keepdims=True)
 
     pl.semaphore_wait(barrier, peers)
+    for d in range(1, hn):
+        pl.semaphore_signal(
+            ready, inc=1, device_id={"head": lax.rem(hd + d, hn)}, device_id_type=pl.DeviceIdType.MESH
+        )
 
     def send_x(g):
         pl.when(q2 | q3 | (lower & (q1 | (q0 & jnp.logical_not(relayed(g))))))(lambda: x_two(g).start())
@@ -189,19 +195,15 @@
         pl.when(odd)(lambda: x_chip(g).start())
         pl.when((q0 | q2) & lower)(lambda: x_three(g).start())
 
-    send_x(0)
-
     for o in range(1, STEPS):
         pl.when(me >= o)(lambda o=o: st_send(o).start())
 
-    @pl.loop(1, chunks)
+    @pl.loop(0, chunks)
     def _(g):
         send_x(g)
 
-    @pl.loop(0, chunks)
-    def _(g):
-        load_k(g).start()
-        load_v(g).start()
+    load_k.start()
+    load_v.start()
 
     for o in range(1, STEPS):
 
@@ -236,21 +238,19 @@
             x_chip(g).wait_recv()
 
         pl.when(has2)(lambda: x_relay(g).wait_recv())
-        load_k(g).wait()
-        load_v(g).wait()
         allowed = lax.broadcasted_iota(jnp.int32, (kbr, STEPS * qb), 0) <= offrow[...]
         for h in range(hc):
             c = slice(h * dh, (h + 1) * dh)
             qh = x[g, 0, :, c]
             doh = x[g, 1, :, c]
-            kh = kb[g, :, c]
-            vh = vb[g, :, c]
+            out = pl.ds(pl.multiple_of(g * w + h * dh, dh), dh)
+            kh = kb[:, out]
+            vh = vb[:, out]
             row = pl.ds(g * hc + h, 1)
             s = dot(kh, qh, 1, 1) * scale - lse[row, :]
             p = jnp.where(allowed, jnp.exp(s), 0.0)
             dp = dot(vh, doh, 1, 1)
             ds = (p * (dp - dlt[row, :]) * scale).astype(BF16)
-            out = pl.ds(pl.multiple_of(g * w + h * dh, dh), dh)
             vgb[:, out] = dot(p.astype(BF16), doh, 1, 0).astype(BF16)
             kgb[:, out] = dot(ds, qh, 1, 0).astype(BF16)
             dq = dot(ds, kh, 0, 0)
@@ -274,24 +274,10 @@
     def finish(g):
         for d in range(hn):
             hs = lax.rem(hd + d, hn)
-            if d:
-                arrived(0, g, hs).wait()
-                total = mate[0, hs, g].astype(F32)
-            else:
-                total = own[g, pl.ds(piece(hd), rows_out), :]
-            here = pl.ds(pl.multiple_of(hs * feats + g * w, w), w)
-
-            @pl.when(toc)
-            def _():
-                arrived(1, g, hs).wait()
-
-            @pl.when(to2)
-            def _():
-                arrived(2, g, hs).wait()
-
+            total = mate[0, hs, g].astype(F32) if d else own[g, pl.ds(piece(hd), rows_out), :]
             total = total + jnp.where(toc, mate[1, hs, g].astype(F32), 0.0)
             total = total + jnp.where(to2, mate[2, hs, g].astype(F32), 0.0)
-            outb[:, here] = total.astype(BF16)
+            outb[:, pl.ds(pl.multiple_of(hs * feats + g * w, w), w)] = total.astype(BF16)
 
     for g in range(min(AHEAD, chunks)):
         forward(g)
@@ -304,8 +290,13 @@
         dlt[:, o * qb:(o + 1) * qb] = st[o, :, qb:2 * qb]
 
     def sent(t):
-        below = jnp.clip((t - WAIT0) * RATE0, 0, t - LAG0)
-        return jnp.clip(jnp.where((quad < 2) & (me + 4 < n), below, t - LAG1), 0, chunks)
+        low = jnp.where(me + 4 < n, jnp.clip((t - WAIT0) * RATE0, 0, t - LAG0), t - LAG0)
+        high = jnp.clip((t - WAIT1) * RATE1, 0, t - LAG1)
+        return jnp.clip(jnp.where(quad < 2, low, high), 0, chunks)
+
+    pl.semaphore_wait(ready, hn - 1)
+    load_k.wait()
+    load_v.wait()
 
     @pl.loop(1, chunks + 1)
     def _(t):
@@ -321,29 +312,37 @@
     def _(g):
         combine(g)
 
-    @pl.loop(0, chunks)
-    def _(g):
-        pl.when(q2 | q3 | lower)(lambda: x_two(g).wait_send())
-        pl.when(odd | lower)(lambda: x_chip(g).wait_send())
-        pl.when(q3 & lower & relayed(g))(lambda: via_down(g).wait_send())
-
-        @pl.when(has2)
-        def _():
-            x_relay(g).wait_send()
-            p_partner(g).wait_send()
-
-        for d in range(1, hn):
-            p_own(g, d).wait_send()
-
+    sent_x = x.at[:, :, pl.ds(0, qb)]
+    pl.when(q2 | q3 | lower)(lambda: drain(sent_x, xs.at[0]))
+    pl.when(odd | lower)(lambda: drain(sent_x, xs.at[1]))
+    pl.when(has2)(lambda: drain(x.at[:, :, rows(2)], xs.at[2]))
+    if upto > start:
+        pl.when(q3 & lower)(lambda: drain(via.at[pl.ds(start, upto - start)], xs.at[3]))
+    pl.when(has2)(lambda: drain(part.at[:, rows(oc)], ps))
     for o in range(1, STEPS):
         pl.when(me >= o)(lambda o=o: st_send(o).wait_send())
 
-    @pl.loop(0, chunks)
+    for d in range(hn):
+        hs = lax.rem(hd + d, hn)
+        if d:
+            drain(part.at[:, pl.ds(0, rows_out)], rsnd.at[0, d])
+            drain(mate.at[0, hs], rrcv.at[0, hs])
+        pl.when(hasa)(lambda d=d: drain(part.at[:, pl.ds(0, rows_out)], rsnd.at[1, d]))
+        pl.when(toc)(lambda hs=hs: drain(mate.at[1, hs], rrcv.at[1, hs]))
+        if bulk:
+            pl.when(to2)(lambda hs=hs: drain(mate.at[2, hs, pl.ds(0, bulk)], rrcv.at[2, hs]))
+
+    @pl.loop(0, bulk)
     def _(g):
         finish(g)
-        for d in range(hn):
-            pl.when(hasa)(lambda d=d: p_ahead(g, d).wait_send())
-            pl.when(has2)(lambda d=d: p_two(g, d).wait_send())
+
+    for g in range(bulk, chunks):
+        for hs in range(hn):
+            pl.when(to2)(lambda g=g, hs=hs: drain(mate.at[2, hs, g], rrcv.at[order(2, g), hs]))
+        finish(g)
+
+    for d in range(hn):
+        pl.when(has2)(lambda d=d: drain(part.at[:, pl.ds(0, rows_out)], rsnd.at[2, d]))
 
 
 def write_out(kgb, vgb, outb, kg_hbm, vg_hbm, qg_hbm, sem):
@@ -386,8 +385,8 @@
         scratch_shapes=[
             pltpu.VMEM((chunks, 2, span, w), BF16),
             pltpu.VMEM((chunks, 2, qb, w), BF16),
-            pltpu.VMEM((chunks, kbr, w), BF16),
-            pltpu.VMEM((chunks, kbr, w), BF16),
+            pltpu.VMEM((kbr, feats), BF16),
+            pltpu.VMEM((kbr, feats), BF16),
             pltpu.VMEM((qb, feats), BF16),
             pltpu.VMEM((heads, qb), F32),
             pltpu.VMEM((1, qb), jnp.int32),
@@ -399,10 +398,8 @@
             pltpu.VMEM((chunks, span, w), BF16),
             pltpu.VMEM((chunks, qb, w), BF16),
             pltpu.VMEM((3, hn, chunks, qb // hn, w), BF16),
-            dma((2, chunks)), dma((2, chunks)), dma((3,)),
-            dma((4, chunks)), dma((4, chunks)), dma((3,)), dma((3,)),
-            dma((chunks,)), dma((chunks,)),
-            dma((3, hn, chunks)), dma((3, hn, chunks)),
+            dma((6,)), dma((4,)), dma((4, chunks)), dma((3,)), dma((3,)),
+            dma(()), dma((chunks,)), dma((3, hn)), dma((5, hn)), pltpu.SemaphoreType.REGULAR,
         ],
         compiler_params=pltpu.CompilerParams(
             collective_id=0, has_side_effects=True, vmem_limit_bytes=40 * 1024 * 1024

time: 33.5 us -> 31.9 us (0.952)
  Pallas kernels: 32.7 us -> 30.9 us
    pallas_call x1, Pallas kernels: 31.1 us -> 29.3 us  [per_device(): pl.pallas_call(functools.partial(kernel, dims), out_shape=tuple((pltpu.VM...]
where the time goes in v3:
time: 31.9 us; the launch traced here: 31.5 us
  Pallas kernels  30.9 us (97%)
  between operations  0.64 us (2%)
    pallas_call x1, Pallas kernels, per_device(): pl.pallas_call(functools.partial(kernel, dims), out_shape=tuple((pltpu.VM...  29.3 us
    pallas_call x1, Pallas kernels, per_device(): pl.pallas_call(write_out, out_shape=outs, in_specs=[pl.BlockSpec(memory_s...  1.62 us

profile of v3, /device:TPU:8, one launch (start us, length us, event | category | flops | bytes accessed | tf_op | source)
XLA Modules:
  0.0 31.5 jit_solution(7154885613957586515)
XLA Ops:
  0.6 29.3 %shard_map.94 = (bf16[256,2560]{1,0:T(8,128)(2,1)S(1)}, bf16[256,2560]{1,0:T(8,128)(2,1)S(1)}, bf16[32,5120]{1,0:T(8,128)(2,1)S(1)}) custom-call(bf16[64,2560]{1,0:T(8,128)(2,1)} %q_hbm.1, s32[1,64]{1,0:T(1,128)} %bitcast.1, bf16[64,2560]{1,0:T(8,128)(2,1)} %o_hbm.1, bf16[64,2560]{1,0:T(8,128)(2,1)} %do_hbm.1, f32[20,64]{1,0:T(8,128)} %ln_hbm.1, ...), custom_call_target="tpu_custom_call" | custom-call | tf_op jit(solution)/shard_map/pallas_call | solution.py:380
  29.9 1.6 %shard_map.95 = (bf16[256,2560]{1,0:T(8,128)(2,1)}, bf16[256,2560]{1,0:T(8,128)(2,1)}, bf16[32,5120]{1,0:T(8,128)(2,1)}) custom-call(bf16[256,2560]{1,0:T(8,128)(2,1)S(1)} %get-tuple-element.6.kgb, bf16[256,2560]{1,0:T(8,128)(2,1)S(1)} %get-tuple-element.7.vgb, bf16[32,5120]{1,0:T(8,128)(2,1)S(1)} %get-tuple-element.8.outb), custom_call_target="tpu_custom_call" | custom-call | tf_op jit(solution)/shard_map/pallas_call | solution.py:408

commit v4 on v3

--- a/solution.py
+++ b/solution.py
@@ -12,10 +12,10 @@
 HEADS_PER_CHUNK = 2
 LAG0 = 1
 LAG1 = 1
-WAIT1 = 0
-RATE1 = 9
-WAIT0 = 5
-RATE0 = 2
+WAIT1 = 2
+RATE1 = 3
+WAIT0 = 6
+RATE0 = 3
 FROM = 2
 UPTO = 8
 AHEAD = 3
@@ -30,7 +30,7 @@
 def kernel(
     dims, q_hbm, off_hbm, o_hbm, do_hbm, ln_hbm, k_hbm, v_hbm,
     kgb, vgb, outb,
-    x, via, kb, vb, ob, lnb, offb, st, lse, dlt, offrow, own, part, got, mate,
+    x, via, kb, vb, ob, lnb, offb, st, lse, dlt, offrow, own, part, got, mate, pb, db,
     small_sem, xs, xr, ss, sr, ps, pr, rsnd, rrcv, ready,
 ):
     n, hn, heads, hc, dh, qb, kbr = dims
@@ -170,10 +170,24 @@
     load_ln.start()
     load_off.start()
 
+    drain(x.at[:, :, pl.ds(0, qb)], small_sem.at[3])
+
+    pl.semaphore_wait(barrier, peers)
+    for d in range(1, hn):
+        pl.semaphore_signal(
+            ready, inc=1, device_id={"head": lax.rem(hd + d, hn)}, device_id_type=pl.DeviceIdType.MESH
+        )
+
+    def send_x(g):
+        pl.when(q2 | q3 | (lower & (q1 | (q0 & jnp.logical_not(relayed(g))))))(lambda: x_two(g).start())
+        pl.when(q0 & lower & relayed(g))(lambda: x_side(g).start())
+        pl.when(odd)(lambda: x_chip(g).start())
+        pl.when((q0 | q2) & lower)(lambda: x_three(g).start())
+
+    send_x(0)
+
     load_o.wait()
     load_ln.wait()
-
-    drain(x.at[:, :, pl.ds(0, qb)], small_sem.at[3])
 
     st[0, :, 0:qb] = lnb[...]
     eye = lax.broadcasted_iota(jnp.int32, (qb, qb), 0) == lax.broadcasted_iota(jnp.int32, (qb, qb), 1)
@@ -183,22 +197,10 @@
         t = dot(oh, doh, 1, 1)
         st[0, h:h + 1, qb:2 * qb] = jnp.sum(jnp.where(eye, t, 0.0), axis=0, keepdims=True)
 
-    pl.semaphore_wait(barrier, peers)
-    for d in range(1, hn):
-        pl.semaphore_signal(
-            ready, inc=1, device_id={"head": lax.rem(hd + d, hn)}, device_id_type=pl.DeviceIdType.MESH
-        )
-
-    def send_x(g):
-        pl.when(q2 | q3 | (lower & (q1 | (q0 & jnp.logical_not(relayed(g))))))(lambda: x_two(g).start())
-        pl.when(q0 & lower & relayed(g))(lambda: x_side(g).start())
-        pl.when(odd)(lambda: x_chip(g).start())
-        pl.when((q0 | q2) & lower)(lambda: x_three(g).start())
-
     for o in range(1, STEPS):
         pl.when(me >= o)(lambda o=o: st_send(o).start())
 
-    @pl.loop(0, chunks)
+    @pl.loop(1, chunks)
     def _(g):
         send_x(g)
 
@@ -238,22 +240,24 @@
             x_chip(g).wait_recv()
 
         pl.when(has2)(lambda: x_relay(g).wait_recv())
-        allowed = lax.broadcasted_iota(jnp.int32, (kbr, STEPS * qb), 0) <= offrow[...]
+        half = 2 * qb
+        allowed = lax.broadcasted_iota(jnp.int32, (kbr, half), 0) <= offrow[:, 0:half]
         for h in range(hc):
             c = slice(h * dh, (h + 1) * dh)
-            qh = x[g, 0, :, c]
-            doh = x[g, 1, :, c]
             out = pl.ds(pl.multiple_of(g * w + h * dh, dh), dh)
-            kh = kb[:, out]
-            vh = vb[:, out]
             row = pl.ds(g * hc + h, 1)
-            s = dot(kh, qh, 1, 1) * scale - lse[row, :]
-            p = jnp.where(allowed, jnp.exp(s), 0.0)
-            dp = dot(vh, doh, 1, 1)
-            ds = (p * (dp - dlt[row, :]) * scale).astype(BF16)
-            vgb[:, out] = dot(p.astype(BF16), doh, 1, 0).astype(BF16)
-            kgb[:, out] = dot(ds, qh, 1, 0).astype(BF16)
-            dq = dot(ds, kh, 0, 0)
+            s = dot(kb[:, out], x[g, 0, :, c], 1, 1) * scale - lse[row, :]
+            p = jnp.exp(s)
+            p = jnp.concatenate([jnp.where(allowed, p[:, 0:half], 0.0), p[:, half:]], axis=1)
+            pb[h] = p.astype(BF16)
+            dp = dot(vb[:, out], x[g, 1, :, c], 1, 1)
+            db[h] = (p * (dp - dlt[row, :]) * scale).astype(BF16)
+        for h in range(hc):
+            c = slice(h * dh, (h + 1) * dh)
+            out = pl.ds(pl.multiple_of(g * w + h * dh, dh), dh)
+            vgb[:, out] = dot(pb[h], x[g, 1, :, c], 1, 0).astype(BF16)
+            kgb[:, out] = dot(db[h], x[g, 0, :, c], 1, 0).astype(BF16)
+            dq = dot(db[h], kb[:, out], 0, 0)
             own[g, :, c] = dq
             part[g, :, c] = dq.astype(BF16)
         pl.when(has2)(lambda: p_partner(g).start())
@@ -398,6 +402,8 @@
             pltpu.VMEM((chunks, span, w), BF16),
             pltpu.VMEM((chunks, qb, w), BF16),
             pltpu.VMEM((3, hn, chunks, qb // hn, w), BF16),
+            pltpu.VMEM((hc, kbr, span), BF16),
+            pltpu.VMEM((hc, kbr, span), BF16),
             dma((6,)), dma((4,)), dma((4, chunks)), dma((3,)), dma((3,)),
             dma(()), dma((chunks,)), dma((3, hn)), dma((5, hn)), pltpu.SemaphoreType.REGULAR,
         ],

time: 31.9 us -> 31.3 us (0.981)
  Pallas kernels: 30.9 us -> 30.5 us
    pallas_call x1, Pallas kernels: 29.3 us -> 28.9 us  [per_device(): pl.pallas_call(functools.partial(kernel, dims), out_shape=tuple((pltpu.VM...]
where the time goes in v4:
time: 31.3 us; the launch traced here: 31.2 us
  Pallas kernels  30.5 us (97%)
  between operations  0.64 us (2%)
    pallas_call x1, Pallas kernels, per_device(): pl.pallas_call(functools.partial(kernel, dims), out_shape=tuple((pltpu.VM...  28.9 us
    pallas_call x1, Pallas kernels, per_device(): pl.pallas_call(write_out, out_shape=outs, in_specs=[pl.BlockSpec(memory_s...  1.62 us

profile of v4, /device:TPU:8, one launch (start us, length us, event | category | flops | bytes accessed | tf_op | source)
XLA Modules:
  0.0 31.2 jit_solution(17531392123444575897)
XLA Ops:
  0.6 28.9 %shard_map.94 = (bf16[256,2560]{1,0:T(8,128)(2,1)S(1)}, bf16[256,2560]{1,0:T(8,128)(2,1)S(1)}, bf16[32,5120]{1,0:T(8,128)(2,1)S(1)}) custom-call(bf16[64,2560]{1,0:T(8,128)(2,1)} %q_hbm.1, s32[1,64]{1,0:T(1,128)} %bitcast.1, bf16[64,2560]{1,0:T(8,128)(2,1)} %o_hbm.1, bf16[64,2560]{1,0:T(8,128)(2,1)} %do_hbm.1, f32[20,64]{1,0:T(8,128)} %ln_hbm.1, ...), custom_call_target="tpu_custom_call" | custom-call | tf_op jit(solution)/shard_map/pallas_call | solution.py:384
  29.5 1.6 %shard_map.95 = (bf16[256,2560]{1,0:T(8,128)(2,1)}, bf16[256,2560]{1,0:T(8,128)(2,1)}, bf16[32,5120]{1,0:T(8,128)(2,1)}) custom-call(bf16[256,2560]{1,0:T(8,128)(2,1)S(1)} %get-tuple-element.6.kgb, bf16[256,2560]{1,0:T(8,128)(2,1)S(1)} %get-tuple-element.7.vgb, bf16[32,5120]{1,0:T(8,128)(2,1)S(1)} %get-tuple-element.8.outb), custom_call_target="tpu_custom_call" | custom-call | tf_op jit(solution)/shard_map/pallas_call | solution.py:414

commit v5 on v4

--- a/solution.py
+++ b/solution.py
@@ -111,8 +111,9 @@
     def x_relay(g):
         return remote(slot(g, 2), slot(g, oa), xs.at[2], xr.at[2, g], partner)
 
-    def st_send(o):
-        return remote(st.at[0], st.at[o], ss.at[o - 1], sr.at[o - 1], me - o)
+    st_two = remote(st.at[0], st.at[2], ss.at[0], sr.at[0], me - 2)
+    st_near = remote(st.at[0], st.at[oc], ss.at[1], sr.at[1], me - oc)
+    st_relay = remote(st.at[2], st.at[oa], ss.at[2], sr.at[2], partner)
 
     def p_partner(g):
         return remote(part.at[g, rows(oc)], got.at[g], ps, pr.at[g], partner)
@@ -197,8 +198,8 @@
         t = dot(oh, doh, 1, 1)
         st[0, h:h + 1, qb:2 * qb] = jnp.sum(jnp.where(eye, t, 0.0), axis=0, keepdims=True)
 
-    for o in range(1, STEPS):
-        pl.when(me >= o)(lambda o=o: st_send(o).start())
+    pl.when(to2)(lambda: st_two.start())
+    pl.when(toc)(lambda: st_near.start())
 
     @pl.loop(1, chunks)
     def _(g):
@@ -287,8 +288,13 @@
         forward(g)
     relay(0)
 
-    for o in range(1, STEPS):
-        pl.when(me + o < n)(lambda o=o: st_send(o).wait_recv())
+    @pl.when(has2)
+    def _():
+        st_two.wait_recv()
+        st_relay.start()
+
+    pl.when(hasa)(lambda: st_near.wait_recv())
+    pl.when(has2)(lambda: st_relay.wait_recv())
     for o in range(STEPS):
         lse[:, o * qb:(o + 1) * qb] = st[o, :, 0:qb]
         dlt[:, o * qb:(o + 1) * qb] = st[o, :, qb:2 * qb]
@@ -304,8 +310,8 @@
 
     @pl.loop(1, chunks + 1)
     def _(t):
+        pl.when(t < chunks)(lambda: relay(t))
         pl.when(t + AHEAD - 1 < chunks)(lambda: forward(t + AHEAD - 1))
-        pl.when(t < chunks)(lambda: relay(t))
         compute(t - 1)
 
         @pl.loop(sent(t - 1), sent(t))
@@ -323,8 +329,9 @@
     if upto > start:
         pl.when(q3 & lower)(lambda: drain(via.at[pl.ds(start, upto - start)], xs.at[3]))
     pl.when(has2)(lambda: drain(part.at[:, rows(oc)], ps))
-    for o in range(1, STEPS):
-        pl.when(me >= o)(lambda o=o: st_send(o).wait_send())
+    pl.when(to2)(lambda: st_two.wait_send())
+    pl.when(toc)(lambda: st_near.wait_send())
+    pl.when(has2)(lambda: st_relay.wait_send())
 
     for d in range(hn):
         hs = lax.rem(hd + d, hn)

time: 31.3 us -> 31.1 us (level)
  no operation moved by 1% of the time
where the time goes in v5:
time: 31.1 us; the launch traced here: 30.9 us
  Pallas kernels  30.3 us (97%)
  between operations  0.64 us (2%)
    pallas_call x1, Pallas kernels, per_device(): pl.pallas_call(functools.partial(kernel, dims), out_shape=tuple((pltpu.VM...  28.7 us
    pallas_call x1, Pallas kernels, per_device(): pl.pallas_call(write_out, out_shape=outs, in_specs=[pl.BlockSpec(memory_s...  1.62 us

profile of v5, /device:TPU:8, one launch (start us, length us, event | category | flops | bytes accessed | tf_op | source)
XLA Modules:
  0.0 30.9 jit_solution(17550025836345170144)
XLA Ops:
  0.6 28.7 %shard_map.94 = (bf16[256,2560]{1,0:T(8,128)(2,1)S(1)}, bf16[256,2560]{1,0:T(8,128)(2,1)S(1)}, bf16[32,5120]{1,0:T(8,128)(2,1)S(1)}) custom-call(bf16[64,2560]{1,0:T(8,128)(2,1)} %q_hbm.1, s32[1,64]{1,0:T(1,128)} %bitcast.1, bf16[64,2560]{1,0:T(8,128)(2,1)} %o_hbm.1, bf16[64,2560]{1,0:T(8,128)(2,1)} %do_hbm.1, f32[20,64]{1,0:T(8,128)} %ln_hbm.1, ...), custom_call_target="tpu_custom_call" | custom-call | tf_op jit(solution)/shard_map/pallas_call | solution.py:391
  29.3 1.6 %shard_map.95 = (bf16[256,2560]{1,0:T(8,128)(2,1)}, bf16[256,2560]{1,0:T(8,128)(2,1)}, bf16[32,5120]{1,0:T(8,128)(2,1)}) custom-call(bf16[256,2560]{1,0:T(8,128)(2,1)S(1)} %get-tuple-element.6.kgb, bf16[256,2560]{1,0:T(8,128)(2,1)S(1)} %get-tuple-element.7.vgb, bf16[32,5120]{1,0:T(8,128)(2,1)S(1)} %get-tuple-element.8.outb), custom_call_target="tpu_custom_call" | custom-call | tf_op jit(solution)/shard_map/pallas_call | solution.py:421

commit v6 on v5

--- a/solution.py
+++ b/solution.py
@@ -262,7 +262,7 @@
             own[g, :, c] = dq
             part[g, :, c] = dq.astype(BF16)
         pl.when(has2)(lambda: p_partner(g).start())
-        for d in range(hn):
+        for d in reversed(range(hn)):
             pl.when(hasa)(lambda d=d: p_ahead(g, d).start())
             if d:
                 p_own(g, d).start()
@@ -273,7 +273,7 @@
             p_partner(g).wait_recv()
             both = own[g, 2 * qb:3 * qb, :] + got[g].astype(F32)
             part[g, 2 * qb:3 * qb, :] = both.astype(BF16)
-            for d in range(hn):
+            for d in reversed(range(hn)):
                 p_two(g, d).start()
 
     def finish(g):

time: 31.1 us -> 30.9 us (level)
  no operation moved by 1% of the time
where the time goes in v6:
time: 30.9 us; the launch traced here: 30.8 us
  Pallas kernels  30.1 us (97%)
  between operations  0.64 us (2%)
    pallas_call x1, Pallas kernels, per_device(): pl.pallas_call(functools.partial(kernel, dims), out_shape=tuple((pltpu.VM...  28.5 us
    pallas_call x1, Pallas kernels, per_device(): pl.pallas_call(write_out, out_shape=outs, in_specs=[pl.BlockSpec(memory_s...  1.62 us

profile of v6, /device:TPU:8, one launch (start us, length us, event | category | flops | bytes accessed | tf_op | source)
XLA Modules:
  0.0 30.8 jit_solution(8963456652065571836)
XLA Ops:
  0.6 28.5 %shard_map.94 = (bf16[256,2560]{1,0:T(8,128)(2,1)S(1)}, bf16[256,2560]{1,0:T(8,128)(2,1)S(1)}, bf16[32,5120]{1,0:T(8,128)(2,1)S(1)}) custom-call(bf16[64,2560]{1,0:T(8,128)(2,1)} %q_hbm.1, s32[1,64]{1,0:T(1,128)} %bitcast.1, bf16[64,2560]{1,0:T(8,128)(2,1)} %o_hbm.1, bf16[64,2560]{1,0:T(8,128)(2,1)} %do_hbm.1, f32[20,64]{1,0:T(8,128)} %ln_hbm.1, ...), custom_call_target="tpu_custom_call" | custom-call | tf_op jit(solution)/shard_map/pallas_call | solution.py:391
  29.1 1.6 %shard_map.95 = (bf16[256,2560]{1,0:T(8,128)(2,1)}, bf16[256,2560]{1,0:T(8,128)(2,1)}, bf16[32,5120]{1,0:T(8,128)(2,1)}) custom-call(bf16[256,2560]{1,0:T(8,128)(2,1)S(1)} %get-tuple-element.6.kgb, bf16[256,2560]{1,0:T(8,128)(2,1)S(1)} %get-tuple-element.7.vgb, bf16[32,5120]{1,0:T(8,128)(2,1)S(1)} %get-tuple-element.8.outb), custom_call_target="tpu_custom_call" | custom-call | tf_op jit(solution)/shard_map/pallas_call | solution.py:421
